TPU v7x, 32 devices: a whole 2x2x4 slice. The times are simulated.
32 devices in a mesh: rows: 32 (over z, y, x, core).
Axes of the slice: x: 2, y: 2, z: 4, core: 2. Of those that a mesh axis runs over, the one named last changes fastest.
Arguments:
- adj_diag: int32 [512, 512], P('rows'), may hold values from -2147483648 to 2147483647
- adj_right: int32 [512, 512], P('rows'), may hold values from -2147483648 to 2147483647
- alive_diag: int32 [512, 512], P('rows'), may hold values from -2147483648 to 2147483647
- alive_right: int32 [512, 512], P('rows'), may hold values from -2147483648 to 2147483647
- truss_k: int32 [1], replicated, may hold values from 130 to 193
Outputs:
- support_field: float32 [16384, 1024], P('rows')
- removed_counts: int32 [3], replicated
All inputs are finite; a program needn't handle non-finite values.
Results may differ from a plain program's by a relative error of at most 0.0003.
Values may be sent and summed in bfloat16 or wider, within the bound.
A program may use at most 64 MiB of HBM per device.

v0:
```python
import jax
import jax.numpy as jnp
from jax import lax
from jax.sharding import PartitionSpec as P

ITERS = 3


def shifted(array, axis, by):
    count = lax.axis_size(axis)
    return lax.ppermute(array, axis, [(i, (i + by) % count) for i in range(count)])


def unpack_tile(packed):
    shifts = jnp.arange(32, dtype=jnp.int32)
    tile_bits = packed[:, None, :] >> shifts[None, :, None] & 1
    return tile_bits.reshape(packed.shape[0] * 32, packed.shape[1])


def pack_bits(tile_bits):
    shifts = jnp.arange(32, dtype=jnp.int32)
    sectioned = tile_bits.reshape(tile_bits.shape[0] // 32, 32, tile_bits.shape[1])
    return jnp.sum(sectioned << shifts[None, :, None], axis=1, dtype=jnp.int32)


def within_tile(packed):
    upper_half = jnp.triu(unpack_tile(packed), 1)
    return (upper_half + upper_half.T).astype(jnp.bfloat16)


def across_tile(packed):
    return unpack_tile(packed).astype(jnp.bfloat16)


def pack_across(across):
    return pack_bits(across.astype(jnp.int32))


def fold_within(within):
    width = within.shape[0]
    half = width // 2
    row_ids = lax.broadcasted_iota(jnp.int32, (half, width), 0)
    col_ids = lax.broadcasted_iota(jnp.int32, (half, width), 1)
    flipped = within[half:][::-1, ::-1]
    folded = jnp.where(col_ids > row_ids, within[:half], flipped)
    return pack_bits(folded.astype(jnp.int32))


def unfold_within(packed):
    folded = unpack_tile(packed)
    half = folded.shape[0]
    width = folded.shape[1]
    row_ids = lax.broadcasted_iota(jnp.int32, (half, width), 0)
    col_ids = lax.broadcasted_iota(jnp.int32, (half, width), 1)
    top_rows = jnp.where(col_ids > row_ids, folded, jnp.zeros_like(folded))
    bottom_rows = jnp.where(col_ids < row_ids, folded, jnp.zeros_like(folded))[::-1, ::-1]
    upper_half = jnp.concatenate([top_rows, bottom_rows], axis=0)
    return (upper_half + upper_half.T).astype(jnp.bfloat16)


def support_within(prev_across, within, across):
    inside = lax.dot_general(
        prev_across, prev_across, (((0,), (0,)), ((), ())), preferred_element_type=jnp.float32
    )
    inside = inside + jnp.dot(within, within, preferred_element_type=jnp.float32)
    return inside + lax.dot_general(
        across, across, (((1,), (1,)), ((), ())), preferred_element_type=jnp.float32
    )


def support_across(within, across, next_within):
    between = jnp.dot(within, across, preferred_element_type=jnp.float32)
    return between + jnp.dot(across, next_within, preferred_element_type=jnp.float32)


def keep_edges(support, tile_mask, thresh):
    return jnp.where(support >= thresh, tile_mask, jnp.zeros_like(tile_mask))


def peel(prev_across, within, across, next_within, thresh):
    inside = support_within(prev_across, within, across)
    between = support_across(within, across, next_within)
    return (
        inside,
        between,
        keep_edges(inside, within, thresh),
        keep_edges(between, across, thresh),
    )


def tally(within, new_within, across, new_across):
    removed = jnp.sum((within - new_within).astype(jnp.int32)) // 2
    removed = removed + jnp.sum((across - new_across).astype(jnp.int32))
    return removed


def on_device(adj_diag, adj_right, alive_diag, alive_right, truss_k):
    within = within_tile(adj_diag & alive_diag)
    across_words = adj_right & alive_right
    across = across_tile(across_words)
    thresh = (truss_k[0] - 2).astype(jnp.float32)
    counts = []
    for step in range(ITERS):
        prev_across = across_tile(shifted(pack_across(across), "rows", 1))
        next_within = unfold_within(shifted(fold_within(within), "rows", -1))
        inside, between, new_within, new_across = peel(
            prev_across, within, across, next_within, thresh
        )
        counts.append(tally(within, new_within, across, new_across))
        within, across = (new_within, new_across)
    stacked = jnp.stack(counts)
    stacked = lax.psum(stacked, "rows")
    support = jnp.concatenate(
        [inside * within.astype(jnp.float32), between * across.astype(jnp.float32)], axis=1
    )
    return (support, stacked)


def solution(mesh):
    in_specs = (P("rows", None), P("rows", None), P("rows", None), P("rows", None), P())
    out_specs = (P("rows", None), P())
    return jax.shard_map(
        on_device, mesh=mesh, in_specs=in_specs, out_specs=out_specs, check_vma=False
    )
```

profile of v0, /device:TPU:12, one launch (start us, length us, event | category | flops | bytes accessed | tf_op | source)
XLA Modules:
  0.0 112.2 jit_solution(5490259086250720770)
XLA Ops:
  0.7 0.8 and.74
  1.5 0.2 fusion.17
  1.7 0.3 copy.7
  2.1 0.3 fusion.14
  2.4 0.9 rev.18
  3.4 0.1 fusion.25
  3.5 0.9 collective-permute-start.1
  4.4 0.4 and_convert_fusion.3
  4.9 1.4 %fusion.47 = f32[512,512]{1,0:T(8,128)} fusion(bf16[512,512]{1,0:T(8,128)(2,1)S(1)} %get-tuple-element.17, bf16[512,512]{1,0:T(8,128)(2,1)S(1)} %get-tuple-element.16), kind=kOutput, calls=%fused_computation.93 | convolution fusion | flops 268435456 | bytes 2097152 | tf_op jit(solution)/shard_map/dot_general | solution.py:72
  7.0 0.1 fusion.34
  7.2 0.8 rev.19
  7.9 1.1 pad_add_fusion
  9.0 2.6 %copy.8 = s32[512,512]{0,1:T(8,128)} copy(s32[512,512]{1,0:T(8,128)} %pad_add_fusion) | data formatting | bytes 2097152 | tf_op jit(solution)/shard_map/concatenate | solution.py:57
  11.6 2.2 %fusion.8 = (s32[16,512]{1,0:T(8,128)S(1)}, bf16[512,512]{1,0:T(8,128)(2,1)S(1)}) fusion(bf16[512,512]{1,0:T(8,128)(2,1)S(1)} %get-tuple-element.16, f32[]{:T(128)} %bitcast.4, f32[512,512]{1,0:T(8,128)} %fusion.47, s32[512,512]{0,1:T(8,128)} %copy.8, s32[256,512]{1,0:T(8,128)S(1)} %rev.19, s32[256,512]{1,0:T(8,128)S(1)} %get-tuple-element.14), kind=kOutput, calls=%fused_computation.25 | convolution fusion | flops 270786560 | bytes 4227076 | tf_op jit(solution)/shard_map/dot_general | solution.py:73
  13.8 0.8 collective-permute-start.4
  14.6 0.5 convolution_bitcast_fusion.2
  15.1 0.4 convolution_add_fusion.8
  15.5 0.5 fusion.7
  16.1 0.9 rev.20
  17.0 0.1 fusion.24
  17.1 2.0 %collective-permute-start.2 = (s32[8,512]{1,0:T(8,128)S(1)}, s32[8,512]{1,0:T(8,128)S(1)}, u32[]{:S(2)}, u32[]{:S(2)}) collective-permute-start(s32[8,512]{1,0:T(8,128)S(1)} %fusion.24), channel_id=1, source_target_pairs={{0,31},{1,0},{2,1},{3,2},{4,3},{5,4},{6,5},{7,6},{8,7},{9,8},{10,9... | collective-permute-start | bytes 49160 | tf_op jit(solution)/shard_map/ppermute | solution.py:11
  19.1 0.5 convolution_bitcast_fusion
  19.6 0.4 convolution_add_fusion.4
  20.0 0.5 fusion.6
  20.5 0.9 rev.22
  21.5 0.1 fusion.23
  21.6 0.6 collective-permute-start.5
  22.2 1.4 %fusion.48 = f32[512,512]{1,0:T(8,128)} fusion(bf16[512,512]{1,0:T(8,128)(2,1)S(1)} %fusion.7, bf16[512,512]{1,0:T(8,128)(2,1)S(1)} %get-tuple-element.21), kind=kOutput, calls=%fused_computation.94 | convolution fusion | flops 268435456 | bytes 2097152 | tf_op jit(solution)/shard_map/dot_general | solution.py:72
  23.6 1.4 %fusion.28 = (s32[256,512]{1,0:T(8,128)}, s32[256,512]{1,0:T(8,128)}, s32[256,512]{1,0:T(8,128)}, s32[256,512]{1,0:T(8,128)S(1)}) fusion(s32[8,512]{1,0:T(8,128)S(1)} %collective-permute-done.5, s32[256]{0:T(256)S(1)} %shift_left.64, s32[8,512]{1,0:T(8,128)S(1)} %collective-permute-done.2), kind=kLoop, calls=%fused_computation.69 | loop fusion | flops 1310720 | bytes 2130944 | tf_op jit(solution)/shard_map/jit(_where)/select_n | solution.py:55
  25.0 3.9 %rev.21 = s32[256,512]{1,0:T(8,128)S(1)} reverse(s32[256,512]{1,0:T(8,128)} %get-tuple-element.18), dimensions={0,1} | reverse | bytes 1048576 | tf_op jit(solution)/shard_map/rev | solution.py:56
  28.9 1.1 pad_add_fusion.1
  30.0 2.6 %copy.9 = s32[512,512]{0,1:T(8,128)} copy(s32[512,512]{1,0:T(8,128)} %pad_add_fusion.1) | data formatting | bytes 2097152 | tf_op jit(solution)/shard_map/concatenate | solution.py:57
  32.5 2.4 %fusion.9 = (s32[16,512]{1,0:T(8,128)S(1)}, bf16[512,512]{1,0:T(8,128)(2,1)S(1)}) fusion(bf16[512,512]{1,0:T(8,128)(2,1)S(1)} %get-tuple-element.21, f32[]{:T(128)} %bitcast.4, f32[512,512]{1,0:T(8,128)} %fusion.48, s32[512,512]{0,1:T(8,128)} %copy.9, s32[256,512]{1,0:T(8,128)S(1)} %rev.21, s32[256,512]{1,0:T(8,128)} %copy-done.1), kind=kOutput, calls=%fused_computation.27 | convolution fusion | flops 270786560 | bytes 4227076 | tf_op jit(solution)/shard_map/dot_general | solution.py:73
  34.9 1.0 collective-permute-start.3
  36.0 3.8 %rev.23 = s32[256,512]{1,0:T(8,128)S(1)} reverse(s32[256,512]{1,0:T(8,128)} %get-tuple-element.11), dimensions={0,1} | reverse | bytes 1048576 | tf_op jit(solution)/shard_map/rev | solution.py:56
  39.7 2.1 %pad_add_fusion.2 = s32[512,512]{1,0:T(8,128)} fusion(s32[256,512]{1,0:T(8,128)S(1)} %rev.23, s32[256,512]{1,0:T(8,128)} %get-tuple-element.10), kind=kLoop, calls=%fused_computation.23 | loop fusion | flops 262144 | bytes 2097152 | tf_op jit(solution)/shard_map/concatenate | solution.py:57
  41.8 2.5 %copy.13 = s32[512,512]{0,1:T(8,128)} copy(s32[512,512]{1,0:T(8,128)} %pad_add_fusion.2) | data formatting | bytes 2097152 | tf_op jit(solution)/shard_map/concatenate | solution.py:57
  44.4 0.4 fusion.49
  44.8 0.6 copy-done
  45.4 0.3 copy-done.3
  45.8 1.5 %convert_multiply_fusion = (f32[512,512]{1,0:T(8,128)}, f32[512,512]{1,0:T(8,128)S(1)}) fusion(bf16[512,512]{1,0:T(8,128)(2,1)S(1)} %get-tuple-element.25, f32[]{:T(128)} %bitcast.4, f32[512,512]{1,0:T(8,128)S(1)} %fusion.49, s32[512,512]{0,1:T(8,128)S(1)} %copy-done.3, s32[256,512]{1,0:T(8,128)S(1)} %rev.23, s32[256,512]{1,0:T(8,128)S(1)} %copy-done), kind=kOutput, calls=%fused_computation.48 | convolution fusion | flops 270532608 | bytes 5767172 | tf_op jit(solution)/shard_map/dot_general | solution.py:73
  47.3 1.5 %convert_reduce_fusion.4 = (s32[]{:T(128)}, s32[]{:T(128)}, s32[]{:T(128)}) fusion(bf16[512,512]{1,0:T(8,128)(2,1)S(1)} %get-tuple-element.21, s32[512]{0:T(512)S(1)} %shift_right_arithmetic.162, s32[16,512]{1,0:T(8,128)S(1)} %and.71, bf16[512,512]{1,0:T(8,128)(2,1)S(1)} %get-tuple-element.25, f32[512,512]{1,0:T(8,128)S(1)} %get-tuple-element.23, f32[]{:T(128)} %bitcast.4), kind=kLoop, calls=%fused_computation.46 | loop fusion | flops 4718589 | bytes 2131984 | tf_op jit(solution)/shard_map/reduce_sum | solution.py:93
  48.8 0.5 convolution_bitcast_fusion.1
  49.2 0.4 convolution_add_fusion.2
  49.7 1.5 %convert_multiply_fusion.1 = (f32[512,512]{1,0:T(8,128)}, f32[512,512]{1,0:T(8,128)S(1)}) fusion(bf16[512,512]{1,0:T(8,128)(2,1)S(1)} %fusion.6, f32[]{:T(128)} %bitcast.4, f32[512,512]{1,0:T(8,128)S(1)} %convolution_add_fusion.2, bf16[512,512]{1,0:T(8,128)(2,1)S(1)} %get-tuple-element.25), kind=kOutput, calls=%fused_computation.49 | convolution fusion | flops 269746176 | bytes 4194308 | tf_op jit(solution)/shard_map/dot_general | solution.py:66
  51.2 1.4 %convert_reduce_fusion.5 = (s32[]{:T(128)}, s32[]{:T(128)}, s32[]{:T(128)}) fusion(bf16[512,512]{1,0:T(8,128)(2,1)S(1)} %get-tuple-element.17, bf16[512,512]{1,0:T(8,128)(2,1)S(1)} %fusion.7, bf16[512,512]{1,0:T(8,128)(2,1)S(1)} %fusion.6, f32[512,512]{1,0:T(8,128)S(1)} %get-tuple-element.27, f32[]{:T(128)} %bitcast.4), kind=kLoop, calls=%fused_computation.47 | loop fusion | flops 2883581 | bytes 2621456 | tf_op jit(solution)/shard_map/reduce_sum | solution.py:92
  62.1 47.3 %psum.7 = s32[3]{0:T(128)} all-reduce(s32[3]{0:T(128)S(1)} %pad_add_fusion.3), channel_id=1, replica_groups=mesh['rows'=32] {'rows'}, use_global_device_ids=true, to_apply=%region_12.13 | all-reduce | flops 3 | bytes 24 | tf_op jit(solution)/shard_map/psum | solution.py:112
  109.4 2.8 %pad_maximum_fusion = f32[512,1024]{1,0:T(8,128)} fusion(f32[512,512]{1,0:T(8,128)} %get-tuple-element.22, f32[512,512]{1,0:T(8,128)S(1)} %copy-done.2), kind=kLoop, calls=%fused_computation | loop fusion | flops 524288 | bytes 4194304 | tf_op jit(solution)/shard_map/concatenate | solution.py:113
  (26 shorter events, 0.4 us)
Async XLA Ops:
  0.6 1.4 %copy-start.4 = (s32[16,512]{1,0:T(8,128)S(1)}, s32[16,512]{1,0:T(8,128)}, u32[]{:S(2)}) copy-start(s32[16,512]{1,0:T(8,128)} %param.6) | copy-start | bytes 98308
  0.6 1.4 %copy-start.5 = (s32[16,512]{1,0:T(8,128)S(1)}, s32[16,512]{1,0:T(8,128)}, u32[]{:S(2)}) copy-start(s32[16,512]{1,0:T(8,128)} %param.8) | copy-start | bytes 98308
  3.5 3.5 %collective-permute-start.1 = (s32[8,512]{1,0:T(8,128)S(1)}, s32[8,512]{1,0:T(8,128)S(1)}, u32[]{:S(2)}, u32[]{:S(2)}) collective-permute-start(s32[8,512]{1,0:T(8,128)S(1)} %fusion.25), channel_id=1, source_target_pairs={{0,31},{1,0},{2,1},{3,2},{4,3},{5,4},{6,5},{7,6},{8,7},{9,8},{10,9... | collective-permute-start | bytes 49160 | tf_op jit(solution)/shard_map/ppermute | solution.py:11
  4.8 9.8 %collective-permute-start = (s32[16,512]{1,0:T(8,128)S(1)}, s32[16,512]{1,0:T(8,128)S(1)}, u32[]{:S(2)}, u32[]{:S(2)}) collective-permute-start(s32[16,512]{1,0:T(8,128)S(1)} %get-tuple-element.9), channel_id=1, source_target_pairs={{0,1},{1,2},{2,3},{3,4},{4,5},{5,6},{6,7},{7,8},{8,9},{9,10},{10,1... | collective-permute-start | bytes 98312 | tf_op jit(solution)/shard_map/ppermute | solution.py:11
  13.8 5.3 %collective-permute-start.4 = (s32[16,512]{1,0:T(8,128)S(1)}, s32[16,512]{1,0:T(8,128)S(1)}, u32[]{:S(2)}, u32[]{:S(2)}) collective-permute-start(s32[16,512]{1,0:T(8,128)S(1)} %get-tuple-element.20), channel_id=1, source_target_pairs={{0,1},{1,2},{2,3},{3,4},{4,5},{5,6},{6,7},{7,8},{8,9},{9,10},{10,1... | collective-permute-start | bytes 98312 | tf_op jit(solution)/shard_map/ppermute | solution.py:11
  17.1 6.4 %collective-permute-start.2 = (s32[8,512]{1,0:T(8,128)S(1)}, s32[8,512]{1,0:T(8,128)S(1)}, u32[]{:S(2)}, u32[]{:S(2)}) collective-permute-start(s32[8,512]{1,0:T(8,128)S(1)} %fusion.24), channel_id=1, source_target_pairs={{0,31},{1,0},{2,1},{3,2},{4,3},{5,4},{6,5},{7,6},{8,7},{9,8},{10,9... | collective-permute-start | bytes 49160 | tf_op jit(solution)/shard_map/ppermute | solution.py:11
  21.6 2.0 %collective-permute-start.5 = (s32[8,512]{1,0:T(8,128)S(1)}, s32[8,512]{1,0:T(8,128)S(1)}, u32[]{:S(2)}, u32[]{:S(2)}) collective-permute-start(s32[8,512]{1,0:T(8,128)S(1)} %fusion.23), channel_id=1, source_target_pairs={{0,31},{1,0},{2,1},{3,2},{4,3},{5,4},{6,5},{7,6},{8,7},{9,8},{10,9... | collective-permute-start | bytes 49160 | tf_op jit(solution)/shard_map/ppermute | solution.py:11
  25.0 5.0 %copy-start.1 = (s32[256,512]{1,0:T(8,128)}, s32[256,512]{1,0:T(8,128)S(1)}, u32[]{:S(2)}) copy-start(s32[256,512]{1,0:T(8,128)S(1)} %get-tuple-element.19) | copy-start | bytes 1572868
  34.9 13.8 %collective-permute-start.3 = (s32[16,512]{1,0:T(8,128)S(1)}, s32[16,512]{1,0:T(8,128)S(1)}, u32[]{:S(2)}, u32[]{:S(2)}) collective-permute-start(s32[16,512]{1,0:T(8,128)S(1)} %get-tuple-element.24), channel_id=1, source_target_pairs={{0,1},{1,2},{2,3},{3,4},{4,5},{5,6},{6,7},{7,8},{8,9},{9,10},{10,1... | collective-permute-start | bytes 98312 | tf_op jit(solution)/shard_map/ppermute | solution.py:11
  44.4 1.0 copy-start
  44.4 1.4 %copy-start.3 = (s32[512,512]{0,1:T(8,128)S(1)}, s32[512,512]{0,1:T(8,128)}, u32[]{:S(2)}) copy-start(s32[512,512]{0,1:T(8,128)} %copy.13) | copy-start | bytes 3145732
  51.2 58.2 %copy-start.2 = (f32[512,512]{1,0:T(8,128)S(1)}, f32[512,512]{1,0:T(8,128)}, u32[]{:S(2)}) copy-start(f32[512,512]{1,0:T(8,128)} %get-tuple-element.26) | copy-start | bytes 3145732
where the time goes:
time: 113 us; the launch traced here: 112 us
  blocking collectives  47.3 us (42%)
  local copies, waits for them, and re-layouts  20.3 us (18%)
  matrix products  14.6 us (13%)
  other arithmetic  13.6 us (12%)
  between operations  11 us (10%)
  starting transfers between devices  5.31 us (5%)
    psum x1, blocking collectives, on_device(): stacked = lax.psum(stacked, 'rows')  47.3 us
    rev x3, local copies, waits for them, and re-layouts, unfold_within(): jnp.where(col_ids < row_ids, folded, jnp.zeros_like(folded))[::-1, ::-1]  8.41 us
    concatenate x3, local copies, waits for them, and re-layouts, unfold_within(): upper_half = jnp.concatenate([top_rows, bottom_rows], axis=0)  7.69 us
    dot_general x3, matrix products, support_across(): jnp.dot(across, next_within, preferred_element_type=jnp.float32)  6.13 us
    ppermute x6, starting transfers between devices, shifted(): lax.ppermute(array, axis, [(i, (i + by) % count) for i in range(count)])  5.31 us
    concatenate x3, other arithmetic, unfold_within(): upper_half = jnp.concatenate([top_rows, bottom_rows], axis=0)  4.27 us
    dot_general x3, matrix products, support_across(): between = jnp.dot(within, across, preferred_element_type=jnp.float32)  3.25 us
    concatenate x1, other arithmetic, on_device(): jnp.concatenate([inside * within.astype(jnp.float32), between * across.as...  2.76 us
  transfers between devices with their start and end apart: 6, of which 0 were waited for; matrix products, arithmetic and copies ran while one was open for 24% of the time, Pallas kernels for 0%

commit v1 on v0

--- a/solution.py
+++ b/solution.py
@@ -109,7 +109,9 @@
         counts.append(tally(within, new_within, across, new_across))
         within, across = (new_within, new_across)
     stacked = jnp.stack(counts)
-    stacked = lax.psum(stacked, "rows")
+    stacked = stacked
+    for hop in (1, 2, 4, 8, 16):
+        stacked = stacked + lax.ppermute(stacked, "rows", [(dev, dev ^ hop) for dev in range(32)])
     support = jnp.concatenate(
         [inside * within.astype(jnp.float32), between * across.astype(jnp.float32)], axis=1
     )

time: 113 us -> 89 us (0.79)
  the two profiles are of different devices: /device:TPU:12 before, /device:TPU:0 now
where the time goes in v1:
time: 89 us; the launch traced here: 88 us
  local copies, waits for them, and re-layouts  20.4 us (23%)
  matrix products  14.6 us (16%)
  other arithmetic  14.2 us (16%)
  starting transfers between devices  13.9 us (16%)
  waiting for transfers between devices  13.9 us (16%)
  between operations  11.1 us (12%)
    ppermute x5, waiting for transfers between devices, on_device(): lax.ppermute(stacked, 'rows', [(dev, dev ^ hop) for dev in range(32)])  13.8 us
    ppermute x6, starting transfers between devices, shifted(): lax.ppermute(array, axis, [(i, (i + by) % count) for i in range(count)])  12.5 us
    rev x3, local copies, waits for them, and re-layouts, unfold_within(): jnp.where(col_ids < row_ids, folded, jnp.zeros_like(folded))[::-1, ::-1]  8.42 us
    concatenate x3, local copies, waits for them, and re-layouts, unfold_within(): upper_half = jnp.concatenate([top_rows, bottom_rows], axis=0)  7.69 us
    dot_general x3, matrix products, support_across(): jnp.dot(across, next_within, preferred_element_type=jnp.float32)  6.13 us
    concatenate x3, other arithmetic, unfold_within(): upper_half = jnp.concatenate([top_rows, bottom_rows], axis=0)  4.27 us
    dot_general x3, matrix products, support_across(): between = jnp.dot(within, across, preferred_element_type=jnp.float32)  3.25 us
    concatenate x1, other arithmetic, on_device(): jnp.concatenate([inside * within.astype(jnp.float32), between * across.as...  2.76 us
  transfers between devices with their start and end apart: 11, of which 4 were waited for; matrix products, arithmetic and copies ran while one was open for 34% of the time, Pallas kernels for 0%

profile of v1, /device:TPU:0, one launch (start us, length us, event | category | flops | bytes accessed | tf_op | source)
XLA Modules:
  0.0 88.0 jit_solution(7774666239345363172)
XLA Ops:
  0.7 0.8 and.74
  1.5 0.2 fusion.17
  1.7 0.3 copy.7
  2.1 0.3 fusion.14
  2.4 0.9 %rev.18 = bf16[256,512]{1,0:T(8,128)(2,1)S(1)} reverse(bf16[256,512]{1,0:T(8,128)(2,1)S(1)} %slice.25), dimensions={0,1} | reverse | bytes 524288 | tf_op jit(solution)/shard_map/rev | solution.py:44
  3.4 0.1 fusion.25
  3.5 6.5 %collective-permute-start.1 = (s32[8,512]{1,0:T(8,128)S(1)}, s32[8,512]{1,0:T(8,128)S(1)}, u32[]{:S(2)}, u32[]{:S(2)}) collective-permute-start(s32[8,512]{1,0:T(8,128)S(1)} %fusion.25), channel_id=1, source_target_pairs={{0,31},{1,0},{2,1},{3,2},{4,3},{5,4},{6,5},{7,6},{8,7},{9,8},{10,9... | collective-permute-start | bytes 49160 | tf_op jit(solution)/shard_map/ppermute | solution.py:11
  9.9 0.4 and_convert_fusion.3
  10.4 1.4 %fusion.47 = f32[512,512]{1,0:T(8,128)} fusion(bf16[512,512]{1,0:T(8,128)(2,1)S(1)} %get-tuple-element.17, bf16[512,512]{1,0:T(8,128)(2,1)S(1)} %get-tuple-element.16), kind=kOutput, calls=%fused_computation.93 | convolution fusion | flops 268435456 | bytes 2097152 | tf_op jit(solution)/shard_map/dot_general | solution.py:72
  12.7 0.8 rev.19
  13.5 1.1 %pad_add_fusion = s32[512,512]{1,0:T(8,128)} fusion(s32[256,512]{1,0:T(8,128)S(1)} %rev.19, s32[256,512]{1,0:T(8,128)S(1)} %get-tuple-element.14), kind=kLoop, calls=%fused_computation.21 | loop fusion | flops 262144 | bytes 2097152 | tf_op jit(solution)/shard_map/concatenate | solution.py:57
  14.5 2.6 %copy.8 = s32[512,512]{0,1:T(8,128)} copy(s32[512,512]{1,0:T(8,128)} %pad_add_fusion) | data formatting | bytes 2097152 | tf_op jit(solution)/shard_map/concatenate | solution.py:57
  17.1 2.2 %fusion.8 = (s32[16,512]{1,0:T(8,128)S(1)}, bf16[512,512]{1,0:T(8,128)(2,1)S(1)}) fusion(bf16[512,512]{1,0:T(8,128)(2,1)S(1)} %get-tuple-element.16, f32[]{:T(128)} %bitcast.4, f32[512,512]{1,0:T(8,128)} %fusion.47, s32[512,512]{0,1:T(8,128)} %copy.8, s32[256,512]{1,0:T(8,128)S(1)} %rev.19, s32[256,512]{1,0:T(8,128)S(1)} %get-tuple-element.14), kind=kOutput, calls=%fused_computation.25 | convolution fusion | flops 270786560 | bytes 4227076 | tf_op jit(solution)/shard_map/dot_general | solution.py:73
  19.4 0.5 convolution_bitcast_fusion.2
  19.9 0.4 convolution_add_fusion.8
  20.4 0.5 fusion.7
  20.9 0.9 %rev.20 = bf16[256,512]{1,0:T(8,128)(2,1)S(1)} reverse(bf16[256,512]{1,0:T(8,128)(2,1)S(1)} %slice.27), dimensions={0,1} | reverse | bytes 524288 | tf_op jit(solution)/shard_map/rev | solution.py:44
  22.0 5.4 %collective-permute-start.2 = (s32[8,512]{1,0:T(8,128)S(1)}, s32[8,512]{1,0:T(8,128)S(1)}, u32[]{:S(2)}, u32[]{:S(2)}) collective-permute-start(s32[8,512]{1,0:T(8,128)S(1)} %fusion.24), channel_id=1, source_target_pairs={{0,31},{1,0},{2,1},{3,2},{4,3},{5,4},{6,5},{7,6},{8,7},{9,8},{10,9... | collective-permute-start | bytes 49160 | tf_op jit(solution)/shard_map/ppermute | solution.py:11
  27.3 0.5 convolution_bitcast_fusion
  27.8 0.4 convolution_add_fusion.4
  28.2 0.5 fusion.6
  28.8 0.9 %rev.22 = bf16[256,512]{1,0:T(8,128)(2,1)S(1)} reverse(bf16[256,512]{1,0:T(8,128)(2,1)S(1)} %slice.29), dimensions={0,1} | reverse | bytes 524288 | tf_op jit(solution)/shard_map/rev | solution.py:44
  29.8 0.5 collective-permute-start.5
  30.4 1.4 %fusion.48 = f32[512,512]{1,0:T(8,128)} fusion(bf16[512,512]{1,0:T(8,128)(2,1)S(1)} %fusion.7, bf16[512,512]{1,0:T(8,128)(2,1)S(1)} %get-tuple-element.21), kind=kOutput, calls=%fused_computation.94 | convolution fusion | flops 268435456 | bytes 2097152 | tf_op jit(solution)/shard_map/dot_general | solution.py:72
  31.8 1.4 %fusion.28 = (s32[256,512]{1,0:T(8,128)}, s32[256,512]{1,0:T(8,128)}, s32[256,512]{1,0:T(8,128)}, s32[256,512]{1,0:T(8,128)S(1)}) fusion(s32[8,512]{1,0:T(8,128)S(1)} %collective-permute-done.5, s32[256]{0:T(256)S(1)} %shift_left.64, s32[8,512]{1,0:T(8,128)S(1)} %collective-permute-done.2), kind=kLoop, calls=%fused_computation.69 | loop fusion | flops 1310720 | bytes 2130944 | tf_op jit(solution)/shard_map/jit(_where)/select_n | solution.py:55
  33.2 3.9 %rev.21 = s32[256,512]{1,0:T(8,128)S(1)} reverse(s32[256,512]{1,0:T(8,128)} %get-tuple-element.18), dimensions={0,1} | reverse | bytes 1048576 | tf_op jit(solution)/shard_map/rev | solution.py:56
  37.1 1.1 %pad_add_fusion.1 = s32[512,512]{1,0:T(8,128)} fusion(s32[256,512]{1,0:T(8,128)S(1)} %rev.21, s32[256,512]{1,0:T(8,128)S(1)} %get-tuple-element.19), kind=kLoop, calls=%fused_computation.22 | loop fusion | flops 262144 | bytes 2097152 | tf_op jit(solution)/shard_map/concatenate | solution.py:57
  38.2 2.6 %copy.9 = s32[512,512]{0,1:T(8,128)} copy(s32[512,512]{1,0:T(8,128)} %pad_add_fusion.1) | data formatting | bytes 2097152 | tf_op jit(solution)/shard_map/concatenate | solution.py:57
  40.7 2.4 %fusion.9 = (s32[16,512]{1,0:T(8,128)S(1)}, bf16[512,512]{1,0:T(8,128)(2,1)S(1)}) fusion(bf16[512,512]{1,0:T(8,128)(2,1)S(1)} %get-tuple-element.21, f32[]{:T(128)} %bitcast.4, f32[512,512]{1,0:T(8,128)} %fusion.48, s32[512,512]{0,1:T(8,128)} %copy.9, s32[256,512]{1,0:T(8,128)S(1)} %rev.21, s32[256,512]{1,0:T(8,128)} %copy-done.1), kind=kOutput, calls=%fused_computation.27 | convolution fusion | flops 270786560 | bytes 4227076 | tf_op jit(solution)/shard_map/dot_general | solution.py:73
  43.2 3.8 %rev.23 = s32[256,512]{1,0:T(8,128)S(1)} reverse(s32[256,512]{1,0:T(8,128)} %get-tuple-element.11), dimensions={0,1} | reverse | bytes 1048576 | tf_op jit(solution)/shard_map/rev | solution.py:56
  47.0 2.1 %pad_add_fusion.2 = s32[512,512]{1,0:T(8,128)} fusion(s32[256,512]{1,0:T(8,128)S(1)} %rev.23, s32[256,512]{1,0:T(8,128)} %get-tuple-element.10), kind=kLoop, calls=%fused_computation.23 | loop fusion | flops 262144 | bytes 2097152 | tf_op jit(solution)/shard_map/concatenate | solution.py:57
  49.1 2.5 %copy.13 = s32[512,512]{0,1:T(8,128)} copy(s32[512,512]{1,0:T(8,128)} %pad_add_fusion.2) | data formatting | bytes 2097152 | tf_op jit(solution)/shard_map/concatenate | solution.py:57
  51.7 0.4 fusion.49
  52.1 0.6 copy-done
  52.7 0.3 copy-done.3
  53.0 1.5 %convert_multiply_fusion = (f32[512,512]{1,0:T(8,128)}, f32[512,512]{1,0:T(8,128)S(1)}) fusion(bf16[512,512]{1,0:T(8,128)(2,1)S(1)} %get-tuple-element.25, f32[]{:T(128)} %bitcast.4, f32[512,512]{1,0:T(8,128)S(1)} %fusion.49, s32[512,512]{0,1:T(8,128)S(1)} %copy-done.3, s32[256,512]{1,0:T(8,128)S(1)} %rev.23, s32[256,512]{1,0:T(8,128)S(1)} %copy-done), kind=kOutput, calls=%fused_computation.48 | convolution fusion | flops 270532608 | bytes 5767172 | tf_op jit(solution)/shard_map/dot_general | solution.py:73
  54.5 1.5 %convert_reduce_fusion.4 = (s32[]{:T(128)}, s32[]{:T(128)}, s32[]{:T(128)}) fusion(bf16[512,512]{1,0:T(8,128)(2,1)S(1)} %get-tuple-element.21, s32[512]{0:T(512)S(1)} %shift_right_arithmetic.162, s32[16,512]{1,0:T(8,128)S(1)} %and.71, bf16[512,512]{1,0:T(8,128)(2,1)S(1)} %get-tuple-element.25, f32[512,512]{1,0:T(8,128)S(1)} %get-tuple-element.23, f32[]{:T(128)} %bitcast.4), kind=kLoop, calls=%fused_computation.46 | loop fusion | flops 4718589 | bytes 2131984 | tf_op jit(solution)/shard_map/reduce_sum | solution.py:93
  56.0 0.5 convolution_bitcast_fusion.1
  56.5 0.4 convolution_add_fusion.2
  57.0 1.5 %convert_multiply_fusion.1 = (f32[512,512]{1,0:T(8,128)}, f32[512,512]{1,0:T(8,128)S(1)}) fusion(bf16[512,512]{1,0:T(8,128)(2,1)S(1)} %fusion.6, f32[]{:T(128)} %bitcast.4, f32[512,512]{1,0:T(8,128)S(1)} %convolution_add_fusion.2, bf16[512,512]{1,0:T(8,128)(2,1)S(1)} %get-tuple-element.25), kind=kOutput, calls=%fused_computation.49 | convolution fusion | flops 269746176 | bytes 4194308 | tf_op jit(solution)/shard_map/dot_general | solution.py:66
  58.4 1.4 %convert_reduce_fusion.5 = (s32[]{:T(128)}, s32[]{:T(128)}, s32[]{:T(128)}) fusion(bf16[512,512]{1,0:T(8,128)(2,1)S(1)} %get-tuple-element.17, bf16[512,512]{1,0:T(8,128)(2,1)S(1)} %fusion.7, bf16[512,512]{1,0:T(8,128)(2,1)S(1)} %fusion.6, f32[512,512]{1,0:T(8,128)S(1)} %get-tuple-element.27, f32[]{:T(128)} %bitcast.4), kind=kLoop, calls=%fused_computation.47 | loop fusion | flops 2883581 | bytes 2621456 | tf_op jit(solution)/shard_map/reduce_sum | solution.py:92
  69.4 2.8 %pad_maximum_fusion = f32[512,1024]{1,0:T(8,128)} fusion(f32[512,512]{1,0:T(8,128)} %get-tuple-element.22, f32[512,512]{1,0:T(8,128)S(1)} %copy-done.2), kind=kLoop, calls=%fused_computation | loop fusion | flops 524288 | bytes 4194304 | tf_op jit(solution)/shard_map/concatenate | solution.py:115
  72.2 3.6 %collective-permute-done.7 = s32[3]{0:T(128)S(1)} collective-permute-done((s32[3]{0:T(128)S(1)}, s32[3]{0:T(128)S(1)}, u32[]{:S(2)}, u32[]{:S(2)}) %collective-permute-start.7) | collective-permute-done | bytes 44 | tf_op jit(solution)/shard_map/ppermute | solution.py:114
  75.9 3.6 %collective-permute-done.8 = s32[3]{0:T(128)S(1)} collective-permute-done((s32[3]{0:T(128)S(1)}, s32[3]{0:T(128)S(1)}, u32[]{:S(2)}, u32[]{:S(2)}) %collective-permute-start.8) | collective-permute-done | bytes 44 | tf_op jit(solution)/shard_map/ppermute | solution.py:114
  79.4 3.6 %collective-permute-done.9 = s32[3]{0:T(128)S(1)} collective-permute-done((s32[3]{0:T(128)S(1)}, s32[3]{0:T(128)S(1)}, u32[]{:S(2)}, u32[]{:S(2)}) %collective-permute-start.9) | collective-permute-done | bytes 44 | tf_op jit(solution)/shard_map/ppermute | solution.py:114
  83.0 1.3 %collective-permute-start.10 = (s32[3]{0:T(128)S(1)}, s32[3]{0:T(128)S(1)}, u32[]{:S(2)}, u32[]{:S(2)}) collective-permute-start(s32[3]{0:T(128)S(1)} %add.87), channel_id=1, source_target_pairs={{0,16},{1,17},{2,18},{3,19},{4,20},{5,21},{6,22},{7,23},{8,24},{9,... | collective-permute-start | bytes 44 | tf_op jit(solution)/shard_map/ppermute | solution.py:114
  84.3 3.2 %collective-permute-done.10 = s32[3]{0:T(128)S(1)} collective-permute-done((s32[3]{0:T(128)S(1)}, s32[3]{0:T(128)S(1)}, u32[]{:S(2)}, u32[]{:S(2)}) %collective-permute-start.10) | collective-permute-done | bytes 44 | tf_op jit(solution)/shard_map/ppermute | solution.py:114
  87.5 0.5 add.88
  (40 shorter events, 1.1 us)
Async XLA Ops:
  0.6 1.4 %copy-start.4 = (s32[16,512]{1,0:T(8,128)S(1)}, s32[16,512]{1,0:T(8,128)}, u32[]{:S(2)}) copy-start(s32[16,512]{1,0:T(8,128)} %param.6) | copy-start | bytes 98308
  0.6 1.4 %copy-start.5 = (s32[16,512]{1,0:T(8,128)S(1)}, s32[16,512]{1,0:T(8,128)}, u32[]{:S(2)}) copy-start(s32[16,512]{1,0:T(8,128)} %param.8) | copy-start | bytes 98308
  3.5 9.1 %collective-permute-start.1 = (s32[8,512]{1,0:T(8,128)S(1)}, s32[8,512]{1,0:T(8,128)S(1)}, u32[]{:S(2)}, u32[]{:S(2)}) collective-permute-start(s32[8,512]{1,0:T(8,128)S(1)} %fusion.25), channel_id=1, source_target_pairs={{0,31},{1,0},{2,1},{3,2},{4,3},{5,4},{6,5},{7,6},{8,7},{9,8},{10,9... | collective-permute-start | bytes 49160 | tf_op jit(solution)/shard_map/ppermute | solution.py:11
  10.3 9.1 %collective-permute-start = (s32[16,512]{1,0:T(8,128)S(1)}, s32[16,512]{1,0:T(8,128)S(1)}, u32[]{:S(2)}, u32[]{:S(2)}) collective-permute-start(s32[16,512]{1,0:T(8,128)S(1)} %get-tuple-element.9), channel_id=1, source_target_pairs={{0,1},{1,2},{2,3},{3,4},{4,5},{5,6},{6,7},{7,8},{8,9},{9,10},{10,1... | collective-permute-start | bytes 98312 | tf_op jit(solution)/shard_map/ppermute | solution.py:11
  19.4 8.0 %collective-permute-start.4 = (s32[16,512]{1,0:T(8,128)S(1)}, s32[16,512]{1,0:T(8,128)S(1)}, u32[]{:S(2)}, u32[]{:S(2)}) collective-permute-start(s32[16,512]{1,0:T(8,128)S(1)} %get-tuple-element.20), channel_id=1, source_target_pairs={{0,1},{1,2},{2,3},{3,4},{4,5},{5,6},{6,7},{7,8},{8,9},{9,10},{10,1... | collective-permute-start | bytes 98312 | tf_op jit(solution)/shard_map/ppermute | solution.py:11
  22.0 9.8 %collective-permute-start.2 = (s32[8,512]{1,0:T(8,128)S(1)}, s32[8,512]{1,0:T(8,128)S(1)}, u32[]{:S(2)}, u32[]{:S(2)}) collective-permute-start(s32[8,512]{1,0:T(8,128)S(1)} %fusion.24), channel_id=1, source_target_pairs={{0,31},{1,0},{2,1},{3,2},{4,3},{5,4},{6,5},{7,6},{8,7},{9,8},{10,9... | collective-permute-start | bytes 49160 | tf_op jit(solution)/shard_map/ppermute | solution.py:11
  29.8 2.0 %collective-permute-start.5 = (s32[8,512]{1,0:T(8,128)S(1)}, s32[8,512]{1,0:T(8,128)S(1)}, u32[]{:S(2)}, u32[]{:S(2)}) collective-permute-start(s32[8,512]{1,0:T(8,128)S(1)} %fusion.23), channel_id=1, source_target_pairs={{0,31},{1,0},{2,1},{3,2},{4,3},{5,4},{6,5},{7,6},{8,7},{9,8},{10,9... | collective-permute-start | bytes 49160 | tf_op jit(solution)/shard_map/ppermute | solution.py:11
  33.2 5.0 %copy-start.1 = (s32[256,512]{1,0:T(8,128)}, s32[256,512]{1,0:T(8,128)S(1)}, u32[]{:S(2)}) copy-start(s32[256,512]{1,0:T(8,128)S(1)} %get-tuple-element.19) | copy-start | bytes 1572868
  43.1 12.9 %collective-permute-start.3 = (s32[16,512]{1,0:T(8,128)S(1)}, s32[16,512]{1,0:T(8,128)S(1)}, u32[]{:S(2)}, u32[]{:S(2)}) collective-permute-start(s32[16,512]{1,0:T(8,128)S(1)} %get-tuple-element.24), channel_id=1, source_target_pairs={{0,1},{1,2},{2,3},{3,4},{4,5},{5,6},{6,7},{7,8},{8,9},{9,10},{10,1... | collective-permute-start | bytes 98312 | tf_op jit(solution)/shard_map/ppermute | solution.py:11
  51.6 1.0 %copy-start = (s32[256,512]{1,0:T(8,128)S(1)}, s32[256,512]{1,0:T(8,128)}, u32[]{:S(2)}) copy-start(s32[256,512]{1,0:T(8,128)} %get-tuple-element.10) | copy-start | bytes 1572868
  51.6 1.4 %copy-start.3 = (s32[512,512]{0,1:T(8,128)S(1)}, s32[512,512]{0,1:T(8,128)}, u32[]{:S(2)}) copy-start(s32[512,512]{0,1:T(8,128)} %copy.13) | copy-start | bytes 3145732
  58.4 10.9 %copy-start.2 = (f32[512,512]{1,0:T(8,128)S(1)}, f32[512,512]{1,0:T(8,128)}, u32[]{:S(2)}) copy-start(f32[512,512]{1,0:T(8,128)} %get-tuple-element.26) | copy-start | bytes 3145732
  69.3 2.8 %collective-permute-start.6 = (s32[3]{0:T(128)S(1)}, s32[3]{0:T(128)S(1)}, u32[]{:S(2)}, u32[]{:S(2)}) collective-permute-start(s32[3]{0:T(128)S(1)} %pad_add_fusion.3), channel_id=1, source_target_pairs={{0,1},{1,0},{2,3},{3,2},{4,5},{5,4},{6,7},{7,6},{8,9},{9,8},{10,11... | collective-permute-start | bytes 44 | tf_op jit(solution)/shard_map/ppermute | solution.py:114
  72.2 3.6 %collective-permute-start.7 = (s32[3]{0:T(128)S(1)}, s32[3]{0:T(128)S(1)}, u32[]{:S(2)}, u32[]{:S(2)}) collective-permute-start(s32[3]{0:T(128)S(1)} %fusion.71), channel_id=1, source_target_pairs={{0,2},{1,3},{2,0},{3,1},{4,6},{5,7},{6,4},{7,5},{8,10},{9,11},{10,... | collective-permute-start | bytes 44 | tf_op jit(solution)/shard_map/ppermute | solution.py:114
  75.9 3.6 %collective-permute-start.8 = (s32[3]{0:T(128)S(1)}, s32[3]{0:T(128)S(1)}, u32[]{:S(2)}, u32[]{:S(2)}) collective-permute-start(s32[3]{0:T(128)S(1)} %fusion.72), channel_id=1, source_target_pairs={{0,4},{1,5},{2,6},{3,7},{4,0},{5,1},{6,2},{7,3},{8,12},{9,13},{10,... | collective-permute-start | bytes 44 | tf_op jit(solution)/shard_map/ppermute | solution.py:114
  79.4 3.6 %collective-permute-start.9 = (s32[3]{0:T(128)S(1)}, s32[3]{0:T(128)S(1)}, u32[]{:S(2)}, u32[]{:S(2)}) collective-permute-start(s32[3]{0:T(128)S(1)} %add.86), channel_id=1, source_target_pairs={{0,8},{1,9},{2,10},{3,11},{4,12},{5,13},{6,14},{7,15},{8,0},{9,1},... | collective-permute-start | bytes 44 | tf_op jit(solution)/shard_map/ppermute | solution.py:114
  83.0 4.5 %collective-permute-start.10 = (s32[3]{0:T(128)S(1)}, s32[3]{0:T(128)S(1)}, u32[]{:S(2)}, u32[]{:S(2)}) collective-permute-start(s32[3]{0:T(128)S(1)} %add.87), channel_id=1, source_target_pairs={{0,16},{1,17},{2,18},{3,19},{4,20},{5,21},{6,22},{7,23},{8,24},{9,... | collective-permute-start | bytes 44 | tf_op jit(solution)/shard_map/ppermute | solution.py:114
